TPU v7x, 32 devices: a whole 2x2x4 slice. The times are simulated.
32 devices in a mesh: band: 8 (over z, x), dir: 4 (over y, core).
Axes of the slice: x: 2, y: 2, z: 4, core: 2. Of those that a mesh axis runs over, the one named last changes fastest.
Arguments:
- visibilities: bfloat16 [16, 32, 2, 256, 256], P('band', 'dir'), as said below
- sky_model: bfloat16 [16, 32, 2, 256, 256], P('band', 'dir')
- rfi_flags: int32 [16, 8, 8], P('band'), may hold values from 0 to 1, as said below
- destination: int32 [16], P('band'), may hold values from 0 to 15, as said below
Outputs:
- delivered: float32 [16, 32, 2, 256], P('band', 'dir')
- coefficients: float32 [9, 32, 2, 256], P(None, 'dir')
- norm_values: float32 [2, 2], replicated
Inputs may be any that keep to these rules, and one draw needn't show every extreme that they name: `rfi_flags`: 1 marks a flagged baseline block; the share of flagged blocks tends to fall with the subband index. destination holds every row of 0 to 15 once. With the rows split into 8 aligned blocks of 2 rows, one row of block i goes to a row of block i + 1 and the other to a row of block i + 4, modulo 16 // 2. `visibilities`: visibilities follow the model under unknown station gains, with noise.
All inputs are finite; a program needn't handle non-finite values.
Results may differ from a plain program's by a relative error of at most 0.0003.
Values sent between devices are 32-bit elements; how exact they have to be, the bound alone decides.
A program may use at most 128 MiB of HBM per device.

v0:
```python
import jax
import jax.numpy as jnp
from jax import lax
from jax.sharding import PartitionSpec as P

BLOCK = 32
DEGREE = 8
SWEEPS = 4
ITERS = 2


highest = lax.Precision.HIGHEST
penalty_share = 0.4


def from_behind(block, axis, distance):
    devices = range(lax.axis_size(axis))
    route = [((i - distance) % len(devices), i) for i in devices]
    return lax.ppermute(block, axis, route)


def block_weights(rfi_flags):
    blocks = rfi_flags.shape[-1]
    kept_blocks = (1 - rfi_flags).astype(jnp.float32)
    leading = kept_blocks.shape[:-2]
    spread = jnp.broadcast_to(
        kept_blocks[..., :, None, :, None], leading + (blocks, BLOCK, blocks, BLOCK)
    )
    stations = blocks * BLOCK
    spread = spread.reshape(leading + (stations, stations))
    return spread * (1.0 - jnp.eye(stations, dtype=jnp.float32))


def operators(visibilities, sky_model, rfi_flags):
    baseline = block_weights(rfi_flags)[..., None, :, :]
    data_re = visibilities[..., 0, :, :].astype(jnp.float32)
    data_im = visibilities[..., 1, :, :].astype(jnp.float32)
    model_re = sky_model[..., 0, :, :].astype(jnp.float32)
    model_im = sky_model[..., 1, :, :].astype(jnp.float32)
    oper_re = baseline * (model_re * data_re + model_im * data_im)
    oper_im = baseline * (model_re * data_im - model_im * data_re)
    square = baseline * (model_re * model_re + model_im * model_im)
    return (jnp.stack([oper_re, oper_im], axis=-3), square)


def chebyshev(band_rows, band_total):
    abscissa = (2.0 * band_rows + 1.0) / band_total - 1.0
    cheb_terms = [jnp.ones_like(abscissa), abscissa]
    for degree in range(2, DEGREE + 1):
        cheb_terms.append(2.0 * abscissa * cheb_terms[-1] - cheb_terms[-2])
    return jnp.stack(cheb_terms[: DEGREE + 1], axis=0)


def stefcal(operator, square, gain_now, target, penalty):
    pen_term = penalty[..., None, None, None]
    for sweep_index in range(SWEEPS):
        products = jnp.einsum("...kapq,...kbq->...kabp", operator, gain_now, precision=highest)
        real_part = products[..., 0, 0, :] - products[..., 1, 1, :]
        imag_part = products[..., 0, 1, :] + products[..., 1, 0, :]
        numerator = jnp.stack([real_part, imag_part], axis=-2)
        magnitude = jnp.sum(gain_now * gain_now, axis=-2)
        denominator = jnp.einsum("...kpq,...kq->...kp", square, magnitude, precision=highest)
        updated = (numerator + pen_term * target) / (denominator[..., None, :] + pen_term)
        gain_now = 0.5 * (updated + gain_now) if sweep_index % 2 == 1 else updated
    return gain_now


def per_device(visibilities, sky_model, rfi_flags, destination):
    local_bands = visibilities.shape[0]
    local_dirs = visibilities.shape[1]
    stations = visibilities.shape[-1]
    blocks = rfi_flags.shape[-1]
    band_index = lax.axis_index("band")
    band_count = lax.axis_size("band")
    band_total = local_bands * band_count
    operator, square = operators(visibilities, sky_model, rfi_flags)
    weights = (1.0 + jnp.sum(1 - rfi_flags, axis=(1, 2)).astype(jnp.float32)) / (
        1.0 + blocks * blocks
    )
    penalty = penalty_share * stations * weights
    band_rows = (band_index * local_bands + jnp.arange(local_bands)).astype(jnp.float32)
    cheb_basis = chebyshev(band_rows, band_total)
    weighted = cheb_basis * weights[None, :]
    gram_part = jnp.dot(weighted, cheb_basis.T, precision=highest)
    ones_part = jnp.ones((local_bands, local_dirs, stations), jnp.float32)
    unit_gains = jnp.stack([ones_part, jnp.zeros_like(ones_part)], axis=2)
    gain_now = unit_gains
    consensus = unit_gains
    dual_var = jnp.zeros_like(unit_gains)
    row_weight = weights[:, None, None, None]
    norm_rows = []
    gram_matrix = gram_part
    coefficients = None
    for iteration in range(ITERS):
        gain_now = stefcal(operator, square, gain_now, consensus - dual_var, penalty)
        projection = jnp.einsum("cs,skap->ckap", weighted, gain_now + dual_var, precision=highest)
        projection, gram_matrix = lax.psum((projection, gram_part), "band")
        factor = jnp.linalg.cholesky(gram_matrix)
        flat_proj = projection.reshape(projection.shape[0], -1)
        coefficients = jax.scipy.linalg.cho_solve((factor, True), flat_proj).reshape(
            projection.shape
        )
        fresh_gains = jnp.einsum("cs,ckap->skap", cheb_basis, coefficients, precision=highest)
        dual_var = dual_var + gain_now - fresh_gains
        local_terms = jnp.stack(
            [
                jnp.sum(row_weight * (gain_now - fresh_gains) ** 2),
                jnp.sum(row_weight * (fresh_gains - consensus) ** 2),
            ]
        )
        consensus = fresh_gains
        norm_rows.append(lax.psum(local_terms, ("band", "dir")))
    totals = jnp.stack(norm_rows)
    normalizer = local_dirs * lax.axis_size("dir") * 2.0 * stations * gram_matrix[0, 0]
    norm_values = jnp.sqrt(totals / normalizer)
    flat_gains = gain_now.reshape(local_bands, -1)
    dest_float = destination.astype(jnp.float32)
    near_gains, near_dest = from_behind((flat_gains, dest_float), "band", 1)
    far_gains, far_dest = from_behind((flat_gains, dest_float), "band", band_count // 2)
    all_gains = jnp.concatenate([flat_gains, near_gains, far_gains], axis=0)
    all_dest = jnp.concatenate([dest_float, near_dest, far_dest], axis=0)
    selector = (all_dest[None, :] == band_rows[:, None]).astype(jnp.float32)
    delivered = jnp.dot(selector, all_gains, precision=highest)
    return (delivered.reshape(gain_now.shape), coefficients, norm_values)


def solution(mesh):
    return jax.shard_map(
        per_device,
        mesh=mesh,
        in_specs=(
            P("band", "dir", None, None, None),
            P("band", "dir", None, None, None),
            P("band", None, None),
            P("band"),
        ),
        out_specs=(P("band", "dir", None, None), P(None, "dir", None, None), P()),
        check_vma=False,
    )
```

profile of v0, /device:TPU:0, one launch (start us, length us, event | category | flops | bytes accessed | tf_op | source)
XLA Modules:
  0.0 308.3 jit_solution(2496416499271665687)
XLA Ops:
  7.9 4.1 %collective-permute-start.1 = (f32[2]{0:T(128)S(1)}, f32[2]{0:T(128)S(1)}, u32[]{:S(2)}, u32[]{:S(2)}) collective-permute-start(f32[2]{0:T(128)S(1)} %convert_element_type.93), channel_id=1, source_target_pairs={{16,0},{20,4},{24,8},{28,12},{0,16},{4,20},{8,24},{12,28},{17,1},{... | collective-permute-start | bytes 32 | tf_op jit(solution)/shard_map/ppermute | solution.py:19
  11.9 1.5 collective-permute-start
  15.3 6.7 %fusion.91 = f32[2,8,1,256]{3,2,1,0:T(1,128)S(1)} fusion(f32[2,256,256]{2,1,0:T(8,128)S(1)} %broadcast_multiply_fusion, bf16[2,8,2,256,256]{4,3,2,1,0:T(8,128)(2,1)} %param.8), kind=kOutput, calls=%fused_computation.155 | convolution fusion | flops 18874368 | bytes 4734976 | tf_op jit(solution)/shard_map/...kpq,...kq->...kp/dot_general | solution.py:62
  22.0 1.9 fusion.1
  24.0 6.9 %fusion.107 = f32[2,8,2,2,256]{4,2,3,1,0:T(2,128)S(1)} fusion(f32[2,8,2,256,1]{3,2,4,1,0:T(2,128)S(1)} %copy-done.10, f32[2,8,1,256,256]{4,3,2,1,0:T(8,128)S(1)} %get-tuple-element.29, f32[2,8,1,256,256]{4,3,2,1,0:T(8,128)S(1)} %get-tuple-element.28), kind=kOutput, calls=%fused_computation.194 | convolution fusion | flops 52428800 | bytes 8486912 | tf_op jit(solution)/shard_map/...kapq,...kbq->...kabp/dot_general | solution.py:57
  31.1 4.4 %fusion.79 = f32[2,8,1,256]{3,2,1,0:T(1,128)S(1)} fusion(f32[2,8,256,1]{2,1,0,3:T(8,128)S(1)} %bitcast.186, f32[2,256,256]{2,1,0:T(8,128)S(1)} %broadcast_multiply_fusion, bf16[2,8,2,256,256]{4,3,2,1,0:T(8,128)(2,1)S(1)} %copy-done.6), kind=kOutput, calls=%fused_computation.142 | convolution fusion | flops 18874368 | bytes 4751360 | tf_op jit(solution)/shard_map/...kpq,...kq->...kp/dot_general | solution.py:62
  35.6 7.1 %fusion.45 = f32[2,8,2,2,256]{4,2,3,1,0:T(2,128)S(1)} fusion(f32[2,8,2,256,1]{3,1,2,0,4:T(8,128)S(1)} %bitcast.170, f32[2,8,1,256,256]{4,3,2,1,0:T(8,128)S(1)} %get-tuple-element.29, f32[2,8,1,256,256]{4,3,2,1,0:T(8,128)S(1)} %get-tuple-element.28), kind=kOutput, calls=%fused_computation.71 | convolution fusion | flops 52428800 | bytes 8486912 | tf_op jit(solution)/shard_map/...kapq,...kbq->...kabp/dot_general | solution.py:57
  42.8 4.4 %fusion.77 = f32[2,8,1,256]{3,2,1,0:T(1,128)S(1)} fusion(f32[2,8,256,1]{2,1,0,3:T(8,128)S(1)} %bitcast.182, f32[2,256,256]{2,1,0:T(8,128)S(1)} %broadcast_multiply_fusion, bf16[2,8,2,256,256]{4,3,2,1,0:T(8,128)(2,1)S(1)} %copy-done.6), kind=kOutput, calls=%fused_computation.140 | convolution fusion | flops 18874368 | bytes 4751360 | tf_op jit(solution)/shard_map/...kpq,...kq->...kp/dot_general | solution.py:62
  47.2 7.3 %fusion.43 = f32[2,8,2,2,256]{4,2,3,1,0:T(2,128)S(1)} fusion(f32[2,8,2,256,1]{3,1,2,0,4:T(8,128)S(1)} %bitcast.179, f32[2,8,1,256,256]{4,3,2,1,0:T(8,128)S(1)} %get-tuple-element.29, f32[2,8,1,256,256]{4,3,2,1,0:T(8,128)S(1)} %get-tuple-element.28), kind=kOutput, calls=%fused_computation.69 | convolution fusion | flops 52428800 | bytes 8486912 | tf_op jit(solution)/shard_map/...kapq,...kbq->...kabp/dot_general | solution.py:57
  54.7 4.4 %fusion.75 = f32[2,8,1,256]{3,2,1,0:T(1,128)S(1)} fusion(f32[2,8,256,1]{2,1,0,3:T(8,128)S(1)} %bitcast.187, f32[2,256,256]{2,1,0:T(8,128)S(1)} %broadcast_multiply_fusion, bf16[2,8,2,256,256]{4,3,2,1,0:T(8,128)(2,1)S(1)} %copy-done.6), kind=kOutput, calls=%fused_computation.138 | convolution fusion | flops 18874368 | bytes 4751360 | tf_op jit(solution)/shard_map/...kpq,...kq->...kp/dot_general | solution.py:62
  59.1 6.9 %fusion.41 = f32[2,8,2,2,256]{4,2,3,1,0:T(2,128)S(1)} fusion(f32[2,8,2,256,1]{3,1,2,0,4:T(8,128)S(1)} %bitcast.168, f32[2,8,1,256,256]{4,3,2,1,0:T(8,128)S(1)} %get-tuple-element.29, f32[2,8,1,256,256]{4,3,2,1,0:T(8,128)S(1)} %get-tuple-element.28), kind=kOutput, calls=%fused_computation.67 | convolution fusion | flops 52428800 | bytes 8486912 | tf_op jit(solution)/shard_map/...kapq,...kbq->...kabp/dot_general | solution.py:57
  67.0 0.8 reshape.456
  68.0 20.9 %psum.38 = f32[9,9]{0,1:T(8,128)S(1)} all-reduce(f32[9,9]{0,1:T(8,128)S(1)} %fusion.95), channel_id=1, replica_groups=mesh['band'=8,'dir'=4] {'band'}, use_global_device_ids=true, to_apply=%region_4.0 | all-reduce | flops 81 | bytes 648 | tf_op jit(solution)/shard_map/psum | solution.py:97
  90.5 1.0 fusion.82
  91.5 6.6 %fusion.73 = f32[2,8,1,256]{3,2,1,0:T(1,128)S(1)} fusion(f32[2,8,256,1]{2,1,0,3:T(8,128)S(1)} %bitcast.181, f32[2,256,256]{2,1,0:T(8,128)S(1)} %broadcast_multiply_fusion, bf16[2,8,2,256,256]{4,3,2,1,0:T(8,128)(2,1)} %param.8), kind=kOutput, calls=%fused_computation.136 | convolution fusion | flops 18874368 | bytes 4751360 | tf_op jit(solution)/shard_map/...kpq,...kq->...kp/dot_general | solution.py:62
  98.2 9.1 %fusion.39 = f32[2,8,2,2,256]{4,2,3,1,0:T(2,128)S(1)} fusion(f32[2,8,2,256,1]{3,1,2,0,4:T(8,128)S(1)} %bitcast.166, f32[2,8,1,256,256]{4,3,2,1,0:T(8,128)} %copy-done.3, f32[2,8,1,256,256]{4,3,2,1,0:T(8,128)S(1)} %copy-done.1), kind=kOutput, calls=%fused_computation.65 | convolution fusion | flops 52428800 | bytes 8486912 | tf_op jit(solution)/shard_map/...kapq,...kbq->...kabp/dot_general | solution.py:57
  109.3 29.9 %all-reduce.4.cloned.1.call-done = f32[9,4096]{1,0:T(8,128)} async-done(((f32[9,4096]{1,0:T(8,128)}), f32[9,4096]{1,0:T(8,128)}) %all-reduce.4.cloned.1.call-update) | async-done | bytes 147472 | tf_op jit(solution)/shard_map/psum | solution.py:97
  139.2 1.4 fusion.87
  141.5 7.0 %fusion.71 = f32[2,8,1,256]{3,2,1,0:T(1,128)S(1)} fusion(f32[2,8,256,1]{2,1,0,3:T(8,128)S(1)} %bitcast.183, f32[2,256,256]{2,1,0:T(8,128)S(1)} %broadcast_multiply_fusion, bf16[2,8,2,256,256]{4,3,2,1,0:T(8,128)(2,1)} %param.8), kind=kOutput, calls=%fused_computation.134 | convolution fusion | flops 18874368 | bytes 4751360 | tf_op jit(solution)/shard_map/...kpq,...kq->...kp/dot_general | solution.py:62
  148.6 6.9 %fusion.37 = f32[2,8,2,2,256]{4,2,3,1,0:T(2,128)S(1)} fusion(f32[2,8,2,256,1]{3,1,2,0,4:T(8,128)S(1)} %bitcast.169, f32[2,8,1,256,256]{4,3,2,1,0:T(8,128)S(1)} %copy-done.4, f32[2,8,1,256,256]{4,3,2,1,0:T(8,128)S(1)} %copy-done.2), kind=kOutput, calls=%fused_computation.63 | convolution fusion | flops 52428800 | bytes 8486912 | tf_op jit(solution)/shard_map/...kapq,...kbq->...kabp/dot_general | solution.py:57
  155.6 4.4 %fusion.69 = f32[2,8,1,256]{3,2,1,0:T(1,128)S(1)} fusion(f32[2,8,256,1]{2,1,0,3:T(8,128)S(1)} %bitcast.184, f32[2,256,256]{2,1,0:T(8,128)S(1)} %broadcast_multiply_fusion, bf16[2,8,2,256,256]{4,3,2,1,0:T(8,128)(2,1)S(1)} %copy-done.7), kind=kOutput, calls=%fused_computation.132 | convolution fusion | flops 18874368 | bytes 4751360 | tf_op jit(solution)/shard_map/...kpq,...kq->...kp/dot_general | solution.py:62
  160.0 7.3 %fusion.35 = f32[2,8,2,2,256]{4,2,3,1,0:T(2,128)S(1)} fusion(f32[2,8,2,256,1]{3,1,2,0,4:T(8,128)S(1)} %bitcast.180, f32[2,8,1,256,256]{4,3,2,1,0:T(8,128)S(1)} %copy-done.4, f32[2,8,1,256,256]{4,3,2,1,0:T(8,128)S(1)} %copy-done.2), kind=kOutput, calls=%fused_computation.61 | convolution fusion | flops 52428800 | bytes 8486912 | tf_op jit(solution)/shard_map/...kapq,...kbq->...kabp/dot_general | solution.py:57
  167.4 4.4 %fusion.67 = f32[2,8,1,256]{3,2,1,0:T(1,128)S(1)} fusion(f32[2,8,256,1]{2,1,0,3:T(8,128)S(1)} %bitcast.185, f32[2,256,256]{2,1,0:T(8,128)S(1)} %broadcast_multiply_fusion, bf16[2,8,2,256,256]{4,3,2,1,0:T(8,128)(2,1)S(1)} %copy-done.7), kind=kOutput, calls=%fused_computation.130 | convolution fusion | flops 18874368 | bytes 4751360 | tf_op jit(solution)/shard_map/...kpq,...kq->...kp/dot_general | solution.py:62
  171.9 7.1 %fusion.33 = f32[2,8,2,2,256]{4,2,3,1,0:T(2,128)S(1)} fusion(f32[2,8,2,256,1]{3,1,2,0,4:T(8,128)S(1)} %bitcast.167, f32[2,8,1,256,256]{4,3,2,1,0:T(8,128)S(1)} %copy-done.4, f32[2,8,1,256,256]{4,3,2,1,0:T(8,128)S(1)} %copy-done.2), kind=kOutput, calls=%fused_computation.59 | convolution fusion | flops 52428800 | bytes 8486912 | tf_op jit(solution)/shard_map/...kapq,...kbq->...kabp/dot_general | solution.py:57
  179.1 1.7 collective-permute-start.3
  180.8 1.4 collective-permute-start.2
  184.0 3.5 %collective-permute-done.2 = f32[2,4096]{1,0:T(2,128)S(1)} collective-permute-done((f32[2,4096]{1,0:T(2,128)S(1)}, f32[2,4096]{1,0:T(2,128)S(1)}, u32[]{:S(2)}, u32[]{:S(2)}) %collective-permute-start.2) | collective-permute-done | bytes 32800 | tf_op jit(solution)/shard_map/ppermute | solution.py:19
  187.7 67.2 %all-reduce.6.cloned.1.call-done = f32[9,4096]{1,0:T(8,128)} async-done(((f32[9,4096]{1,0:T(8,128)}), f32[9,4096]{1,0:T(8,128)}) %all-reduce.6.cloned.1.call-update) | async-done | bytes 147472 | tf_op jit(solution)/shard_map/psum | solution.py:97
  254.9 1.4 fusion.83
  257.9 1.3 maximum_bitcast_fusion.1
  259.2 1.4 maximum_bitcast_fusion
  261.2 39.5 %all-reduce = (f32[1,2]{1,0:T(1,128)S(1)}, f32[1,2]{1,0:T(1,128)S(1)}) all-reduce(f32[1,2]{1,0:T(1,128)S(1)} %maximum_bitcast_fusion.1, f32[1,2]{1,0:T(1,128)S(1)} %maximum_bitcast_fusion), channel_id=1, replica_groups=mesh['band'=8,'dir'=4] {'band','dir'}, use_global_device_ids=true, to_apply=%region_18.0 | all-reduce | flops 4 | bytes 32 | tf_op jit(solution)/shard_map/psum | solution.py:112
  (103 shorter events, 13.4 us)
Async XLA Ops:
  7.2 132.0 %all-reduce.4.cloned.1.call-start = ((), (), s32[]{:S(2)}) async-start(), calls=%async_computation | async-start | bytes 524288 | tf_op jit(solution)/shard_map/psum | solution.py:97
  7.9 101.4 %collective-permute-start.1 = (f32[2]{0:T(128)S(1)}, f32[2]{0:T(128)S(1)}, u32[]{:S(2)}, u32[]{:S(2)}) collective-permute-start(f32[2]{0:T(128)S(1)} %convert_element_type.93), channel_id=1, source_target_pairs={{16,0},{20,4},{24,8},{28,12},{0,16},{4,20},{8,24},{12,28},{17,1},{... | collective-permute-start | bytes 32 | tf_op jit(solution)/shard_map/ppermute | solution.py:19
  11.9 97.3 %collective-permute-start = (f32[2]{0:T(128)S(1)}, f32[2]{0:T(128)S(1)}, u32[]{:S(2)}, u32[]{:S(2)}) collective-permute-start(f32[2]{0:T(128)S(1)} %convert_element_type.93), channel_id=1, source_target_pairs={{28,0},{0,4},{4,8},{8,12},{12,16},{16,20},{20,24},{24,28},{29,1},{... | collective-permute-start | bytes 32 | tf_op jit(solution)/shard_map/ppermute | solution.py:19
  15.2 6.8 %copy-start.6 = (bf16[2,8,2,256,256]{4,3,2,1,0:T(8,128)(2,1)S(1)}, bf16[2,8,2,256,256]{4,3,2,1,0:T(8,128)(2,1)}, u32[]{:S(2)}) copy-start(bf16[2,8,2,256,256]{4,3,2,1,0:T(8,128)(2,1)} %param.8) | copy-start | bytes 12582916
  15.3 6.8 %copy-start.5 = (bf16[2,8,2,256,256]{4,3,2,1,0:T(8,128)(2,1)S(1)}, bf16[2,8,2,256,256]{4,3,2,1,0:T(8,128)(2,1)}, u32[]{:S(2)}) copy-start(bf16[2,8,2,256,256]{4,3,2,1,0:T(8,128)(2,1)} %param.7) | copy-start | bytes 12582916
  22.0 2.0 copy-start.10
  24.0 35.2 %copy-start = (f32[2,8,1,256,256]{4,3,2,1,0:T(8,128)}, f32[2,8,1,256,256]{4,3,2,1,0:T(8,128)S(1)}, u32[]{:S(2)}) copy-start(f32[2,8,1,256,256]{4,3,2,1,0:T(8,128)S(1)} %get-tuple-element.28) | copy-start | bytes 12582916
  24.0 35.1 %copy-start.3 = (f32[2,8,1,256,256]{4,3,2,1,0:T(8,128)}, f32[2,8,1,256,256]{4,3,2,1,0:T(8,128)S(1)}, u32[]{:S(2)}) copy-start(f32[2,8,1,256,256]{4,3,2,1,0:T(8,128)S(1)} %get-tuple-element.29) | copy-start | bytes 12582916
  24.0 7.0 %copy-start.9 = (f32[2,8,2,256]{3,1,2,0:T(8,128)S(1)}, f32[2,8,2,256]{3,1,2,0:T(8,128)}, u32[]{:S(2)}) copy-start(f32[2,8,2,256]{3,1,2,0:T(8,128)} %constant.65.clone.1) | copy-start | bytes 98308
  67.8 187.1 %all-reduce.6.cloned.1.call-start = ((), (), s32[]{:S(2)}) async-start(), calls=%async_computation.1 | async-start | bytes 524288 | tf_op jit(solution)/shard_map/psum | solution.py:97
  89.8 8.4 %copy-start.1 = (f32[2,8,1,256,256]{4,3,2,1,0:T(8,128)S(1)}, f32[2,8,1,256,256]{4,3,2,1,0:T(8,128)}, u32[]{:S(2)}) copy-start(f32[2,8,1,256,256]{4,3,2,1,0:T(8,128)} %copy-done) | copy-start | bytes 12582916
  141.0 7.5 %copy-start.2 = (f32[2,8,1,256,256]{4,3,2,1,0:T(8,128)S(1)}, f32[2,8,1,256,256]{4,3,2,1,0:T(8,128)}, u32[]{:S(2)}) copy-start(f32[2,8,1,256,256]{4,3,2,1,0:T(8,128)} %copy-done) | copy-start | bytes 12582916
  141.1 7.5 %copy-start.4 = (f32[2,8,1,256,256]{4,3,2,1,0:T(8,128)S(1)}, f32[2,8,1,256,256]{4,3,2,1,0:T(8,128)}, u32[]{:S(2)}) copy-start(f32[2,8,1,256,256]{4,3,2,1,0:T(8,128)} %copy-done.3) | copy-start | bytes 12582916
  148.6 7.0 %copy-start.7 = (bf16[2,8,2,256,256]{4,3,2,1,0:T(8,128)(2,1)S(1)}, bf16[2,8,2,256,256]{4,3,2,1,0:T(8,128)(2,1)}, u32[]{:S(2)}) copy-start(bf16[2,8,2,256,256]{4,3,2,1,0:T(8,128)(2,1)} %param.8) | copy-start | bytes 12582916
  171.9 85.2 %copy-start.11 = (f32[2,8,2,256]{3,1,2,0:T(8,128)S(1)}, f32[2,8,2,256]{3,1,2,0:T(8,128)}, u32[]{:S(2)}) copy-start(f32[2,8,2,256]{3,1,2,0:T(8,128)} %constant.76.clone.1) | copy-start | bytes 98308
  179.1 4.9 %collective-permute-start.3 = (f32[2,4096]{1,0:T(2,128)S(1)}, f32[2,4096]{1,0:T(2,128)S(1)}, u32[]{:S(2)}, u32[]{:S(2)}) collective-permute-start(f32[2,4096]{1,0:T(2,128)S(1)} %reshape.458), channel_id=1, source_target_pairs={{16,0},{20,4},{24,8},{28,12},{0,16},{4,20},{8,24},{12,28},{17,1},{... | collective-permute-start | bytes 98312 | tf_op jit(solution)/shard_map/ppermute | solution.py:19
  180.8 6.6 %collective-permute-start.2 = (f32[2,4096]{1,0:T(2,128)S(1)}, f32[2,4096]{1,0:T(2,128)S(1)}, u32[]{:S(2)}, u32[]{:S(2)}) collective-permute-start(f32[2,4096]{1,0:T(2,128)S(1)} %reshape.458), channel_id=1, source_target_pairs={{28,0},{0,4},{4,8},{8,12},{12,16},{16,20},{20,24},{24,28},{29,1},{... | collective-permute-start | bytes 98312 | tf_op jit(solution)/shard_map/ppermute | solution.py:19
  256.7 44.5 %copy-start.8 = (f32[9,8,2,256]{3,2,1,0:T(2,128)}, f32[9,8,2,256]{3,2,1,0:T(2,128)S(1)}, u32[]{:S(2)}) copy-start(f32[9,8,2,256]{3,2,1,0:T(2,128)S(1)} %reshape.461) | copy-start | bytes 442372
Sparse Core Ops, SparseCore 0:
  67.9 71.2 all-reduce.3
  183.9 70.9 all-reduce.5
where the time goes:
time: 313 us; the launch traced here: 308 us
  matrix products  106 us (34%)
  waiting for transfers between devices  101 us (32%)
  blocking collectives  60.4 us (19%)
  between operations  15.4 us (5%)
  other arithmetic  11.9 us (4%)
  starting transfers between devices  8.79 us (3%)
  local copies, waits for them, and re-layouts  4.65 us (1%)
    psum x2, waiting for transfers between devices, per_device(): projection, gram_matrix = lax.psum((projection, gram_part), 'band')  97 us
    dot_general x8, matrix products, stefcal(): jnp.einsum('...kapq,...kbq->...kabp', operator, gain_now, precision=highest)  58.6 us
    dot_general x8, matrix products, stefcal(): jnp.einsum('...kpq,...kq->...kp', square, magnitude, precision=highest)  42.2 us
    psum x1, blocking collectives, per_device(): norm_rows.append(lax.psum(local_terms, ('band', 'dir')))  39.5 us
    psum x1, blocking collectives, per_device(): projection, gram_matrix = lax.psum((projection, gram_part), 'band')  20.9 us
    ppermute x4, starting transfers between devices, from_behind(): return lax.ppermute(block, axis, route)  8.72 us
  transfers between devices with their start and end apart: 6, of which 4 were waited for; matrix products, arithmetic and copies ran while one was open for 25% of the time, Pallas kernels for 0%

commit v1 on v0

v1 whole, which is shorter than its diff:
```python
import functools

import jax
import jax.numpy as jnp
from jax import lax
from jax.experimental import pallas as pl
from jax.experimental.pallas import tpu as pltpu
from jax.sharding import PartitionSpec as P

BLOCK = 32
DEGREE = 8
SWEEPS = 4
ITERS = 2
TERMS = DEGREE + 1
ROWS = 16
LANES = 128

penalty_share = 0.4
f32 = jnp.float32
bf16 = jnp.bfloat16
MESH = pl.DeviceIdType.MESH


def row_of(shape, axis=0):
    return lax.broadcasted_iota(jnp.int32, shape, axis)


def spread(value, shape):
    return jnp.broadcast_to(value, shape)


def left_side(gain):
    row = row_of(gain.shape)
    part = lax.rem(row, 4)
    re = spread(gain[0:1], gain.shape)
    im = spread(gain[1:2], gain.shape)
    zero = jnp.zeros_like(gain)
    first = jnp.where(part == 0, re, jnp.where(part == 1, im, zero))
    second = jnp.where(part == 0, -im, jnp.where(part == 1, re, zero))
    third = jnp.where(part == 2, re * re + im * im, zero)
    sides = []
    for full in (first, second, third):
        lead = full.astype(bf16).astype(f32)
        sides.append(jnp.where(row < 4, lead, full - lead).astype(bf16))
    return jnp.concatenate(sides + sides, axis=1)


def kernel(
    bands,
    dirs,
    vis_hbm,
    sky_hbm,
    flags,
    dest,
    delivered,
    coef,
    norms,
    vis,
    sky,
    oper,
    turned,
    keep,
    wpen,
    meta,
    gains,
    zall,
    uall,
    gtile,
    ttile,
    solve_rows,
    cheb_rows,
    norm_all,
    vis_sem,
    sky_sem,
    meta_send,
    meta_recv,
    gain_send,
    gain_recv,
    norm_send,
    norm_recv,
):
    subs, count, _, stations, _ = vis_hbm.shape
    blocks = flags.shape[-1]
    total = bands * subs
    width = meta.shape[-1]
    me = lax.axis_index("band")
    my_dir = lax.axis_index("dir")
    tile = (8, stations)

    def ahead(distance):
        return lax.rem(me + distance, bands)

    def behind(distance):
        return lax.rem(me + bands - distance, bands)

    def load(pair):
        s, k = divmod(pair, count)
        return (
            pltpu.make_async_copy(vis_hbm.at[s, k], vis.at[pair], vis_sem.at[pair]),
            pltpu.make_async_copy(sky_hbm.at[s, k], sky.at[pair], sky_sem.at[pair]),
        )

    for pair in range(subs * count):
        for copy in load(pair):
            copy.start()

    barrier = pltpu.get_barrier_semaphore()
    for distance in range(1, bands):
        pl.semaphore_signal(
            barrier, inc=1, device_id={"band": ahead(distance)}, device_id_type=MESH
        )
    for distance in range(1, dirs):
        pl.semaphore_signal(
            barrier,
            inc=1,
            device_id={"dir": lax.rem(my_dir + distance, dirs)},
            device_id_type=MESH,
        )

    lane_w = row_of((1, width), 1)
    weight_row = jnp.zeros((1, width), f32)
    dest_rows = []
    for s in range(subs):
        kept = (1 - flags[s]).astype(f32)
        weight = (1.0 + jnp.sum(kept, axis=(0, 1), keepdims=True)) / (1.0 + blocks * blocks)
        wpen[s] = spread(penalty_share * stations * weight, tile)
        weight_row = jnp.where(lane_w == me * subs + s, weight, weight_row)
        dest_rows.append(jnp.full((1, width), dest[s], jnp.int32).astype(f32))
        lane = row_of((1, stations), 1) // BLOCK
        for i in range(blocks):
            shape = (BLOCK, stations)
            across = jnp.zeros((1, stations), f32)
            for j in range(blocks):
                across = jnp.where(lane == j, kept[j : j + 1, i : i + 1], across)
            apart = row_of(shape) + i * BLOCK != row_of(shape, 1)
            keep[s, i * BLOCK : (i + 1) * BLOCK, :] = jnp.where(
                apart, spread(across, shape), 0.0
            )
    meta[me] = jnp.zeros(meta.shape[1:], f32)
    for s in range(subs):
        meta[me, s : s + 1, :] = dest_rows[s]
    meta[me, subs : subs + 1, :] = weight_row

    row = row_of(tile)
    for pair in range(subs * count):
        unit = jnp.where(row == 0, 1.0, jnp.zeros(tile, f32))
        gtile[pair] = unit
        ttile[pair] = unit

    pl.semaphore_wait(barrier, bands - 1 + dirs - 1)

    def meta_copy(slot, distance):
        return pltpu.make_async_remote_copy(
            src_ref=meta.at[slot],
            dst_ref=meta.at[slot],
            send_sem=meta_send.at[distance],
            recv_sem=meta_recv.at[distance],
            device_id={"band": ahead(distance)},
            device_id_type=MESH,
        )

    def gain_copy(it, slot, s, distance):
        return pltpu.make_async_remote_copy(
            src_ref=gains.at[it, slot, s],
            dst_ref=gains.at[it, slot, s],
            send_sem=gain_send.at[it, s, distance],
            recv_sem=gain_recv.at[it, s, distance],
            device_id={"band": ahead(distance)},
            device_id_type=MESH,
        )

    def norm_copy(slot, distance):
        return pltpu.make_async_remote_copy(
            src_ref=norm_all.at[slot],
            dst_ref=norm_all.at[slot],
            send_sem=norm_send.at[distance],
            recv_sem=norm_recv.at[distance],
            device_id={"dir": lax.rem(my_dir + distance, dirs)},
            device_id_type=MESH,
        )

    for distance in range(1, bands):
        meta_copy(me, distance).start()

    square = (stations, stations)
    identity = (row_of(square) == row_of(square, 1)).astype(f32).astype(bf16)

    def build(s):
        def one(k, carry):
            pair = s * count + k
            pltpu.make_async_copy(vis_hbm.at[s, k], vis.at[pair], vis_sem.at[pair]).wait()
            pltpu.make_async_copy(sky_hbm.at[s, k], sky.at[pair], sky_sem.at[pair]).wait()
            slot = lax.rem(k, 2)
            for part, source in enumerate((vis, sky)):
                for j in range(2):
                    turned[slot, 2 * part + j] = lax.dot_general(
                        identity,
                        source[pair, j],
                        (((1,), (1,)), ((), ())),
                        preferred_element_type=f32,
                    )
            for i in range(stations // BLOCK):
                rows = slice(i * BLOCK, (i + 1) * BLOCK)
                baseline = keep[s, rows, :]
                data_re = turned[slot, 0, rows, :]
                data_im = turned[slot, 1, rows, :]
                model_re = turned[slot, 2, rows, :]
                model_im = turned[slot, 3, rows, :]
                parts = (
                    baseline * (model_re * data_re + model_im * data_im),
                    baseline * (model_re * data_im - model_im * data_re),
                    baseline * (model_re * model_re + model_im * model_im),
                )
                for j, full in enumerate(parts):
                    lead = full.astype(bf16)
                    base = j * stations + i * BLOCK
                    oper[pair, base : base + BLOCK, :] = lead
                    base = base + 3 * stations
                    oper[pair, base : base + BLOCK, :] = (full - lead.astype(f32)).astype(bf16)
            return carry

        lax.fori_loop(0, count, one, 0, unroll=2)

    def sweeps(it, s):
        penalty = wpen[s]

        def one(index, held):
            step = jnp.where(lax.rem(index, 2) == 1, 0.5, 1.0).astype(f32)
            fresh = []
            for k in range(count):
                pair = s * count + k
                gain = held[k]
                out = lax.dot_general(
                    left_side(gain),
                    oper[pair],
                    (((1,), (0,)), ((), ())),
                    preferred_element_type=f32,
                )
                out = out + pltpu.roll(out, 4, 0)
                updated = (out + penalty * ttile[pair]) / (spread(out[2:3], tile) + penalty)
                fresh.append(step * updated + (1.0 - step) * gain)
            return tuple(fresh)

        start = tuple(gtile[s * count + k] for k in range(count))
        final = lax.fori_loop(0, SWEEPS, one, start)
        for k in range(count):
            gtile[s * count + k] = final[k]
            gains[it, me, s, k : k + 1, 0:stations] = final[k][0:1]
            gains[it, me, s, k : k + 1, stations : 2 * stations] = final[k][1:2]

    def solve():
        weights = meta[0, subs : subs + 1, :]
        for i in range(1, bands):
            weights = weights + meta[i, subs : subs + 1, :]
        index = row_of((1, width), 1).astype(f32)
        abscissa = (2.0 * index + 1.0) / total - 1.0
        terms = [jnp.ones_like(abscissa), abscissa]
        for degree in range(2, DEGREE + 1):
            terms.append(2.0 * abscissa * terms[-1] - terms[-2])
        shape = (ROWS, width)
        cheb = jnp.zeros(shape, f32)
        for c in range(TERMS):
            cheb = jnp.where(row_of(shape) == c, spread(terms[c], shape), cheb)
        right = cheb * weights
        gram = jnp.zeros((ROWS, LANES), f32)
        for c in range(TERMS):
            column = jnp.sum(right * terms[c], axis=1, keepdims=True)
            gram = jnp.where(row_of(gram.shape, 1) == c, column, gram)
        for c in range(TERMS):
            pivot = gram[c : c + 1, c : c + 1]
            gram_row = gram[c : c + 1, :] / pivot
            right_row = right[c : c + 1, :] / pivot
            column = gram[:, c : c + 1]
            gram = jnp.where(row_of(gram.shape) == c, gram_row, gram - column * gram_row)
            right = jnp.where(row_of(shape) == c, right_row, right - column * right_row)
        cheb = jnp.where(row_of(shape) == ROWS - 1, spread(weights, shape), cheb)
        for f in range(total):
            solve_rows[f] = spread(right[:, f : f + 1], (ROWS, stations))
            cheb_rows[f] = spread(cheb[:, f : f + 1], (ROWS, stations))
        return jnp.sum(weights, axis=1, keepdims=True)

    def consensus(it):
        block = (count, stations)
        sums = []
        for half in range(2):
            lanes = slice(half * stations, (half + 1) * stations)

            def project(i, acc):
                for s in range(subs):
                    value = gains[it, i, s, :, lanes]
                    if it > 0:
                        value = value + uall[i, s, :, lanes]
                    f = i * subs + s
                    acc = tuple(
                        acc[c] + spread(solve_rows[f, c : c + 1, :], block) * value
                        for c in range(TERMS)
                    )
                return acc

            coefs = lax.fori_loop(
                0, bands, project, tuple(jnp.zeros(block, f32) for _ in range(TERMS))
            )
            for c in range(TERMS):
                coef[c, :, lanes] = coefs[c]

            def expand(i, acc):
                primal, dual = acc
                for s in range(subs):
                    f = i * subs + s
                    fresh = spread(cheb_rows[f, 0:1, :], block) * coefs[0]
                    for c in range(1, TERMS):
                        fresh = fresh + spread(cheb_rows[f, c : c + 1, :], block) * coefs[c]
                    weight = spread(cheb_rows[f, ROWS - 1 : ROWS, :], block)
                    gap = gains[it, i, s, :, lanes] - fresh
                    if it > 0:
                        moved = fresh - zall[i, s, :, lanes]
                    else:
                        moved = fresh - (1.0 - half)
                    primal = primal + weight * (gap * gap)
                    dual = dual + weight * (moved * moved)
                    if it < ITERS - 1:
                        if it > 0:
                            uall[i, s, :, lanes] = uall[i, s, :, lanes] + gap
                        else:
                            uall[i, s, :, lanes] = gap
                        zall[i, s, :, lanes] = fresh
                return primal, dual

            zero = jnp.zeros(block, f32)
            sums.append(lax.fori_loop(0, bands, expand, (zero, zero)))
        return [
            jnp.sum(sums[0][j] + sums[1][j], axis=(0, 1), keepdims=True) for j in range(2)
        ]

    norm_tile = jnp.zeros((8, LANES), f32)
    weight_sum = None
    for it in range(ITERS):
        for s in range(subs):
            if it == 0:
                build(s)
            sweeps(it, s)
            for distance in range(1, bands):
                gain_copy(it, me, s, distance).start()
        if it == 0:
            for distance in range(1, bands):
                meta_copy(behind(distance), distance).wait_recv()
            weight_sum = solve()
        for s in range(subs):
            for distance in range(1, bands):
                gain_copy(it, behind(distance), s, distance).wait_recv()
        parts = consensus(it)
        for j in range(2):
            norm_tile = jnp.where(
                row_of(norm_tile.shape) == it * 2 + j, parts[j], norm_tile
            )
        if it < ITERS - 1:
            for s in range(subs):
                target = zall[me, s] - uall[me, s]
                for k in range(count):
                    re = spread(target[k : k + 1, 0:stations], tile)
                    im = spread(target[k : k + 1, stations : 2 * stations], tile)
                    ttile[s * count + k] = jnp.where(
                        row == 0, re, jnp.where(row == 1, im, 0.0)
                    )

    norm_all[my_dir] = norm_tile
    for distance in range(1, dirs):
        norm_copy(my_dir, distance).start()

    for s in range(subs):
        wanted = (me * subs + s).astype(f32)
        block = jnp.zeros((count, 2 * stations), f32)
        for distance in sorted({1, bands // 2}):
            source = behind(distance)
            for r in range(subs):
                here = (meta[source, r : r + 1, 0:LANES] == wanted).astype(f32)
                here = spread(here[:, 0:1], block.shape)
                block = block + here * gains[ITERS - 1, source, r]
        delivered[s] = block

    for distance in range(1, dirs):
        norm_copy(lax.rem(my_dir + dirs - distance, dirs), distance).wait_recv()
    sum_tile = norm_all[0]
    for i in range(1, dirs):
        sum_tile = sum_tile + norm_all[i]
    norms[...] = jnp.sqrt(sum_tile / (count * dirs * 2.0 * stations * weight_sum))

    for distance in range(1, dirs):
        norm_copy(my_dir, distance).wait_send()
    for distance in range(1, bands):
        meta_copy(me, distance).wait_send()
        for it in range(ITERS):
            for s in range(subs):
                gain_copy(it, me, s, distance).wait_send()


def per_device(bands, dirs, visibilities, sky_model, rfi_flags, destination):
    subs, count, _, stations, _ = visibilities.shape
    pairs = subs * count
    total = bands * subs
    width = -(-total // LANES) * LANES
    meta_rows = -(-(subs + 1) // 8) * 8
    vmem = pl.BlockSpec(memory_space=pltpu.VMEM)
    hbm = pl.BlockSpec(memory_space=pl.ANY)
    sem = pltpu.SemaphoreType.DMA
    delivered, coefficients, norms = pl.pallas_call(
        functools.partial(kernel, bands, dirs),
        out_shape=(
            jax.ShapeDtypeStruct((subs, count, 2 * stations), f32),
            jax.ShapeDtypeStruct((TERMS, count, 2 * stations), f32),
            jax.ShapeDtypeStruct((8, LANES), f32),
        ),
        in_specs=[hbm, hbm, vmem, pl.BlockSpec(memory_space=pltpu.SMEM)],
        out_specs=(vmem, vmem, vmem),
        scratch_shapes=[
            pltpu.VMEM((pairs, 2, stations, stations), bf16),
            pltpu.VMEM((pairs, 2, stations, stations), bf16),
            pltpu.VMEM((pairs, 6 * stations, stations), bf16),
            pltpu.VMEM((2, 4, stations, stations), f32),
            pltpu.VMEM((subs, stations, stations), f32),
            pltpu.VMEM((subs, 8, stations), f32),
            pltpu.VMEM((bands, meta_rows, width), f32),
            pltpu.VMEM((ITERS, bands, subs, count, 2 * stations), f32),
            pltpu.VMEM((bands, subs, count, 2 * stations), f32),
            pltpu.VMEM((bands, subs, count, 2 * stations), f32),
            pltpu.VMEM((pairs, 8, stations), f32),
            pltpu.VMEM((pairs, 8, stations), f32),
            pltpu.VMEM((total, ROWS, stations), f32),
            pltpu.VMEM((total, ROWS, stations), f32),
            pltpu.VMEM((dirs, 8, LANES), f32),
            sem((pairs,)),
            sem((pairs,)),
            sem((bands,)),
            sem((bands,)),
            sem((ITERS, subs, bands)),
            sem((ITERS, subs, bands)),
            sem((dirs,)),
            sem((dirs,)),
        ],
        compiler_params=pltpu.CompilerParams(
            collective_id=0, has_side_effects=True, vmem_limit_bytes=56 * 1024 * 1024
        ),
    )(visibilities, sky_model, rfi_flags, destination)
    shape = (count, 2, stations)
    return (
        delivered.reshape((subs,) + shape),
        coefficients.reshape((TERMS,) + shape),
        norms[: 2 * ITERS, 0].reshape(ITERS, 2),
    )


def solution(mesh):
    return jax.shard_map(
        functools.partial(per_device, mesh.shape["band"], mesh.shape["dir"]),
        mesh=mesh,
        in_specs=(
            P("band", "dir", None, None, None),
            P("band", "dir", None, None, None),
            P("band", None, None),
            P("band"),
        ),
        out_specs=(P("band", "dir", None, None), P(None, "dir", None, None), P()),
        check_vma=False,
    )
```

time: 313 us -> 50.8 us (0.16); the launches traced: 308 us -> 50.5 us
  matrix products: 106 us -> 0 us
  waiting for transfers between devices: 101 us -> 0 us
  blocking collectives: 60.4 us -> 0 us
  Pallas kernels: 0 us -> 45.4 us
  between operations: 15.4 us -> 0.64 us
  other arithmetic: 11.9 us -> 0 us
  starting transfers between devices: 8.79 us -> 0 us
    dot_general x22 -> x0, matrix products: 103 us -> none  [the longest x8 58.6 us: stefcal(): jnp.einsum('...kapq,...kbq->...kabp', operator, gain_now, precision=highest)]
    psum x2 -> x0, waiting for transfers between devices: 97 us -> none  [per_device(): projection, gram_matrix = lax.psum((projection, gram_part), 'band')]
    psum x2 -> x0, blocking collectives: 60.4 us -> none  [the longest x1 39.5 us: per_device(): norm_rows.append(lax.psum(local_terms, ('band', 'dir')))]
    pallas_call x0 -> x1, Pallas kernels: none -> 45.4 us  [per_device(): pl.pallas_call(functools.partial(kernel, bands, dirs), out_shape=(jax.Sha...]
    ppermute x4 -> x0, starting transfers between devices: 8.72 us -> none  [from_behind(): return lax.ppermute(block, axis, route)]
    another operation x7 -> x0, other arithmetic: 5.85 us -> none  [the longest x2 2.69 us: per_device(): totals = jnp.stack(norm_rows)]
    ppermute x4 -> x0, waiting for transfers between devices: 3.68 us -> none  [from_behind(): return lax.ppermute(block, axis, route)]
    another operation x4 -> x0, matrix products: 3.44 us -> none  [per_device(): jax.scipy.linalg.cho_solve((factor, True), flat_proj)]
  transfers between devices with their start and end apart: 6 -> 0, of which waited for: 4 -> 0; matrix products, arithmetic and copies ran while one was open for 25% -> 0% of each run, Pallas kernels for 0% -> 0%
where the time goes in v1:
time: 50.8 us; the launch traced here: 50.5 us
  Pallas kernels  45.4 us (89%)
  local copies, waits for them, and re-layouts  4.48 us (9%)
  between operations  0.64 us (1%)
    pallas_call x1, Pallas kernels, per_device(): pl.pallas_call(functools.partial(kernel, bands, dirs), out_shape=(jax.Sha...  45.4 us
    unnamed x2, local copies, waits for them, and re-layouts  3.04 us

profile of v1, /device:TPU:0, one launch (start us, length us, event | category | flops | bytes accessed | tf_op | source)
XLA Modules:
  0.0 50.5 jit_solution(17749562261211623113)
XLA Ops:
  0.6 45.4 %shard_map.67 = (f32[2,8,512]{2,1,0:T(8,128)}, f32[9,8,512]{2,1,0:T(8,128)}, f32[8,128]{1,0:T(8,128)}) custom-call(bf16[2,8,2,256,256]{4,3,2,1,0:T(8,128)(2,1)} %vis_hbm.1, bf16[2,8,2,256,256]{4,3,2,1,0:T(8,128)(2,1)} %sky_hbm.1, s32[2,8,8]{2,1,0:T(8,128)} %flags.1, s32[2]{0:T(128)} %dest.1), custom_call_target="tpu_custom_call" | custom-call | tf_op jit(solution)/shard_map/pallas_call | solution.py:406
  46.0 1.4 %copy.9 = f32[2,8,2,256]{3,2,1,0:T(2,128)} copy(f32[2,8,2,256]{3,1,2,0:T(8,128)} %bitcast.3) | data formatting | bytes 65536
  47.4 1.6 %copy.10 = f32[9,8,2,256]{3,2,1,0:T(2,128)} copy(f32[9,8,2,256]{3,1,2,0:T(8,128)} %bitcast.2) | data formatting | bytes 294912
  49.1 0.8 %slice_reduce_fusion = f32[4]{0:T(128)S(1)} fusion(f32[8,128]{1,0:T(8,128)} %get-tuple-element.8), kind=kLoop, calls=%fused_computation | loop fusion | bytes 32 | tf_op jit(solution)/shard_map/slice | solution.py:448
  49.8 0.6 %reshape_squeeze.3 = f32[2,2]{1,0:T(2,128)} reshape(f32[4]{0:T(128)S(1)} %slice_reduce_fusion) | data formatting | bytes 32 | tf_op jit(solution)/shard_map/reshape;squeeze | solution.py:448

commit v2 on v1

--- a/solution.py
+++ b/solution.py
@@ -143,9 +143,7 @@
 
     row = row_of(tile)
     for pair in range(subs * count):
-        unit = jnp.where(row == 0, 1.0, jnp.zeros(tile, f32))
-        gtile[pair] = unit
-        ttile[pair] = unit
+        ttile[pair] = jnp.where(row == 0, 1.0, jnp.zeros(tile, f32))
 
     pl.semaphore_wait(barrier, bands - 1 + dirs - 1)
 
@@ -199,6 +197,7 @@
                         (((1,), (1,)), ((), ())),
                         preferred_element_type=f32,
                     )
+            sums = [jnp.zeros(tile, f32) for _ in range(3)]
             for i in range(stations // BLOCK):
                 rows = slice(i * BLOCK, (i + 1) * BLOCK)
                 baseline = keep[s, rows, :]
@@ -212,11 +211,17 @@
                     baseline * (model_re * model_re + model_im * model_im),
                 )
                 for j, full in enumerate(parts):
+                    for r in range(0, BLOCK, 8):
+                        sums[j] = sums[j] + full[r : r + 8]
                     lead = full.astype(bf16)
                     base = j * stations + i * BLOCK
                     oper[pair, base : base + BLOCK, :] = lead
                     base = base + 3 * stations
                     oper[pair, base : base + BLOCK, :] = (full - lead.astype(f32)).astype(bf16)
+            re, im, mag = (spread(jnp.sum(x, axis=0, keepdims=True), tile) for x in sums)
+            out = jnp.where(row == 0, re, jnp.where(row == 1, im, 0.0))
+            penalty = wpen[s]
+            gtile[pair] = (out + penalty * ttile[pair]) / (mag + penalty)
             return carry
 
         lax.fori_loop(0, count, one, 0, unroll=2)
@@ -242,7 +247,7 @@
             return tuple(fresh)
 
         start = tuple(gtile[s * count + k] for k in range(count))
-        final = lax.fori_loop(0, SWEEPS, one, start)
+        final = lax.fori_loop(1 if it == 0 else 0, SWEEPS, one, start)
         for k in range(count):
             gtile[s * count + k] = final[k]
             gains[it, me, s, k : k + 1, 0:stations] = final[k][0:1]
@@ -300,8 +305,10 @@
             coefs = lax.fori_loop(
                 0, bands, project, tuple(jnp.zeros(block, f32) for _ in range(TERMS))
             )
-            for c in range(TERMS):
-                coef[c, :, lanes] = coefs[c]
+            if it == ITERS - 1:
+                for c in range(TERMS):
+                    for k in range(count):
+                        coef[c, k, half : half + 1, :] = coefs[c][k : k + 1]
 
             def expand(i, acc):
                 primal, dual = acc
@@ -351,7 +358,9 @@
         parts = consensus(it)
         for j in range(2):
             norm_tile = jnp.where(
-                row_of(norm_tile.shape) == it * 2 + j, parts[j], norm_tile
+                (row_of(norm_tile.shape) == it) & (row_of(norm_tile.shape, 1) == j),
+                parts[j],
+                norm_tile,
             )
         if it < ITERS - 1:
             for s in range(subs):
@@ -376,14 +385,17 @@
                 here = (meta[source, r : r + 1, 0:LANES] == wanted).astype(f32)
                 here = spread(here[:, 0:1], block.shape)
                 block = block + here * gains[ITERS - 1, source, r]
-        delivered[s] = block
+        for k in range(count):
+            delivered[s, k, 0:1, :] = block[k : k + 1, 0:stations]
+            delivered[s, k, 1:2, :] = block[k : k + 1, stations : 2 * stations]
 
     for distance in range(1, dirs):
         norm_copy(lax.rem(my_dir + dirs - distance, dirs), distance).wait_recv()
     sum_tile = norm_all[0]
     for i in range(1, dirs):
         sum_tile = sum_tile + norm_all[i]
-    norms[...] = jnp.sqrt(sum_tile / (count * dirs * 2.0 * stations * weight_sum))
+    final = jnp.sqrt(sum_tile / (count * dirs * 2.0 * stations * weight_sum))
+    norms[...] = final[0:ITERS, 0:2]
 
     for distance in range(1, dirs):
         norm_copy(my_dir, distance).wait_send()
@@ -406,9 +418,9 @@
     delivered, coefficients, norms = pl.pallas_call(
         functools.partial(kernel, bands, dirs),
         out_shape=(
-            jax.ShapeDtypeStruct((subs, count, 2 * stations), f32),
-            jax.ShapeDtypeStruct((TERMS, count, 2 * stations), f32),
-            jax.ShapeDtypeStruct((8, LANES), f32),
+            jax.ShapeDtypeStruct((subs, count, 2, stations), f32),
+            jax.ShapeDtypeStruct((TERMS, count, 2, stations), f32),
+            jax.ShapeDtypeStruct((ITERS, 2), f32),
         ),
         in_specs=[hbm, hbm, vmem, pl.BlockSpec(memory_space=pltpu.SMEM)],
         out_specs=(vmem, vmem, vmem),
@@ -441,12 +453,7 @@
             collective_id=0, has_side_effects=True, vmem_limit_bytes=56 * 1024 * 1024
         ),
     )(visibilities, sky_model, rfi_flags, destination)
-    shape = (count, 2, stations)
-    return (
-        delivered.reshape((subs,) + shape),
-        coefficients.reshape((TERMS,) + shape),
-        norms[: 2 * ITERS, 0].reshape(ITERS, 2),
-    )
+    return delivered, coefficients, norms
 
 
 def solution(mesh):

time: 50.8 us -> 49.2 us (0.969)
  Pallas kernels: 45.4 us -> 44.1 us
    pallas_call x1, Pallas kernels: 45.4 us -> 44.1 us  [per_device(): pl.pallas_call(functools.partial(kernel, bands, dirs), out_shape=(jax.Sha...]
    unnamed x2 -> x3, local copies, waits for them, and re-layouts: 3.04 us -> 4.18 us
    slice x1 -> x0, local copies, waits for them, and re-layouts: 0.79 us -> none  [per_device(): norms[:2 * ITERS, 0].reshape(ITERS, 2)]
    another operation x1 -> x0, local copies, waits for them, and re-layouts: 0.65 us -> none  [per_device(): norms[:2 * ITERS, 0].reshape(ITERS, 2)]
where the time goes in v2:
time: 49.2 us; the launch traced here: 48.9 us
  Pallas kernels  44.1 us (90%)
  local copies, waits for them, and re-layouts  4.18 us (8%)
  between operations  0.64 us (1%)
    pallas_call x1, Pallas kernels, per_device(): pl.pallas_call(functools.partial(kernel, bands, dirs), out_shape=(jax.Sha...  44.1 us
    unnamed x3, local copies, waits for them, and re-layouts  4.18 us

profile of v2, /device:TPU:0, one launch (start us, length us, event | category | flops | bytes accessed | tf_op | source)
XLA Modules:
  0.0 48.9 jit_solution(8796542611864796334)
XLA Ops:
  0.6 44.1 %shard_map.67 = (f32[2,8,2,256]{3,2,1,0:T(2,128)}, f32[9,8,2,256]{3,2,1,0:T(2,128)}, f32[2,2]{1,0:T(2,128)}) custom-call(bf16[2,8,2,256,256]{4,3,2,1,0:T(8,128)(2,1)} %vis_hbm.1, bf16[2,8,2,256,256]{4,3,2,1,0:T(8,128)(2,1)} %sky_hbm.1, s32[2,8,8]{2,1,0:T(8,128)} %flags.1, s32[2]{0:T(128)} %dest.1), custom_call_target="tpu_custom_call" | custom-call | tf_op jit(solution)/shard_map/pallas_call | solution.py:418
  44.8 1.4 %copy.10 = f32[2,8,2,256]{3,2,1,0:T(2,128)} copy(f32[2,8,2,256]{3,2,1,0:T(2,128)} %get-tuple-element.6) | data formatting | bytes 65536
  46.1 1.6 %copy.11 = f32[9,8,2,256]{3,2,1,0:T(2,128)} copy(f32[9,8,2,256]{3,2,1,0:T(2,128)} %get-tuple-element.7) | data formatting | bytes 294912
  47.7 1.2 %copy.12 = f32[2,2]{1,0:T(2,128)} copy(f32[2,2]{1,0:T(2,128)} %get-tuple-element.8) | data formatting | bytes 32
